TPU v7x, 32 devices: a whole 2x2x4 slice. The times are simulated.
32 devices in a mesh: mode: 8 (over y, x, core), tm: 4 (over z).
Axes of the slice: x: 2, y: 2, z: 4, core: 2. Of those that a mesh axis runs over, the one named last changes fastest.
Arguments:
- field: float32 [2, 128, 65536], P(None, 'mode', 'tm'), may hold values from -1.8 to 1.8
- beta: float32 [3, 128], P(None, 'mode'), may hold values from -1 to 1
- quartets: int32 [4, 1024], replicated, may hold values from 0 to 127
- intersections: float32 [1024], replicated, may hold values from -0.12 to 0.12
Outputs:
- field_out: float32 [2, 128, 65536], P(None, 'mode', 'tm')
- errors: float32 [2, 128], P(None, 'mode')
All inputs are finite; a program needn't handle non-finite values.
Results may differ from a plain program's by a relative error of at most 0.0003.
Values sent between devices are 32-bit elements; how exact they have to be, the bound alone decides.
A program may use at most 128 MiB of HBM per device.

v0:
```python
import math
import jax
import jax.numpy as jnp
from jax import lax
from jax.sharding import PartitionSpec as P

RADIX = 256
STEPS = 2
epsilon = 1e-06


def phase_of(offset, slope, curve, frequency):
    return math.pi * offset + 300.0 * slope * frequency + 3000.0 * curve * frequency * frequency


def triple_product(left_field, middle_field, conj_field):
    prod_re = left_field[0] * middle_field[0] - left_field[1] * middle_field[1]
    prod_im = left_field[0] * middle_field[1] + left_field[1] * middle_field[0]
    out_re = prod_re * conj_field[0] + prod_im * conj_field[1]
    out_im = prod_im * conj_field[0] - prod_re * conj_field[1]
    return (out_re, out_im)


def contract(form, first_operand, second_operand):
    return jnp.einsum(form, first_operand, second_operand, precision=lax.Precision.HIGHEST)


def rotate(real_part, imag_part, angle):
    cosine = jnp.cos(angle)
    sine_part = jnp.sin(angle)
    return (real_part * cosine - imag_part * sine_part, real_part * sine_part + imag_part * cosine)


def dft_tables(length):
    positions = lax.iota(jnp.int32, length)
    product = positions[:, None] * positions[None, :] % length
    angle = -2.0 * math.pi / length * product.astype(jnp.float32)
    return (jnp.cos(angle), jnp.sin(angle))


def to_columns(state):
    return lax.all_to_all(state, "tm", split_axis=3, concat_axis=2, tiled=True)


def to_rows(state):
    return lax.all_to_all(state, "tm", split_axis=2, concat_axis=3, tiled=True)


def linear_step(state, beta, table_re, table_im):
    radix_size = table_re.shape[0]
    total_time = radix_size * radix_size
    cols_local = state.shape[3]
    tm_index = lax.axis_index("tm")
    head_re = contract("ka,mab->mkb", table_re, state[0]) - contract(
        "ka,mab->mkb", table_im, state[1]
    )
    head_im = contract("ka,mab->mkb", table_re, state[1]) + contract(
        "ka,mab->mkb", table_im, state[0]
    )
    column = tm_index * cols_local + lax.iota(jnp.int32, cols_local)
    row_position = lax.iota(jnp.int32, radix_size)
    twist = (
        -2.0
        * math.pi
        / total_time
        * (row_position[:, None] * column[None, :] % total_time).astype(jnp.float32)
    )
    head_re, head_im = rotate(head_re, head_im, twist[None])
    turned = lax.all_to_all(
        jnp.stack([head_re, head_im]), "tm", split_axis=2, concat_axis=3, tiled=True
    )
    spec_re = contract("mcb,kb->mck", turned[0], table_re) - contract(
        "mcb,kb->mck", turned[1], table_im
    )
    spec_im = contract("mcb,kb->mck", turned[1], table_re) + contract(
        "mcb,kb->mck", turned[0], table_im
    )
    rows_local = turned.shape[2]
    first_index = tm_index * rows_local + lax.iota(jnp.int32, rows_local)
    wave = first_index[:, None] + radix_size * row_position[None, :]
    signed = jnp.where(wave < total_time // 2, wave, wave - total_time)
    frequency = signed.astype(jnp.float32) / (total_time / 2)
    angle = phase_of(
        beta[0][:, None, None], beta[1][:, None, None], beta[2][:, None, None], frequency[None]
    )
    spec_re, spec_im = rotate(spec_re, spec_im, angle)
    back_re = contract("mck,kb->mcb", spec_re, table_re) + contract(
        "mck,kb->mcb", spec_im, table_im
    )
    back_im = contract("mck,kb->mcb", spec_im, table_re) - contract(
        "mck,kb->mcb", spec_re, table_im
    )
    untwist = (
        2.0
        * math.pi
        / total_time
        * (first_index[:, None] * row_position[None, :] % total_time).astype(jnp.float32)
    )
    back_re, back_im = rotate(back_re, back_im, untwist[None])
    gathered = lax.all_to_all(
        jnp.stack([back_re, back_im]), "tm", split_axis=3, concat_axis=2, tiled=True
    )
    scale = 1.0 / total_time
    out_re = (
        contract("ka,mkb->mab", table_re, gathered[0])
        + contract("ka,mkb->mab", table_im, gathered[1])
    ) * scale
    out_im = (
        contract("ka,mkb->mab", table_re, gathered[1])
        - contract("ka,mkb->mab", table_im, gathered[0])
    ) * scale
    return jnp.stack([out_re, out_im])


def kerr_term(fields, quartets, intersections):
    count = quartets.shape[1]
    block_size = min(512, count)
    blocks = count // block_size
    grouped = quartets.reshape(4, blocks, block_size).transpose(1, 0, 2)
    weights = intersections.reshape(blocks, block_size)
    modes_all = fields.shape[1]
    mode_ids = lax.iota(jnp.int32, modes_all)

    def accumulate(running, block_item):
        indices, weight = block_item
        out_re, out_im = triple_product(
            jnp.take(fields, indices[1], axis=1),
            jnp.take(fields, indices[2], axis=1),
            jnp.take(fields, indices[3], axis=1),
        )
        owner = (indices[0][None, :] == mode_ids[:, None]).astype(jnp.float32) * weight[None, :]
        add_re = contract("pq,qt->pt", owner, -out_im)
        add_im = contract("pq,qt->pt", owner, out_re)
        return (running + jnp.stack([add_re, add_im]), None)

    running, unused = lax.scan(accumulate, jnp.zeros_like(fields), (grouped, weights))
    return running


def kerr_step(flat, quartets, intersections):
    spread = lax.all_to_all(flat, "mode", split_axis=2, concat_axis=1, tiled=True)
    first = kerr_term(spread, quartets, intersections)
    second = kerr_term(spread + first, quartets, intersections)
    updated = spread + 0.5 * (first + second)
    estimate = 0.5 * (second - first)
    returned, estimate_home = (
        lax.all_to_all(updated, "mode", split_axis=1, concat_axis=2, tiled=True),
        lax.all_to_all(estimate, "mode", split_axis=1, concat_axis=2, tiled=True),
    )
    error_part = jnp.sum(estimate_home * estimate_home, axis=(0, 2))
    field_part = jnp.sum(returned * returned, axis=(0, 2))
    return (returned, error_part, field_part)


def shards(field, beta, quartets, intersections):
    modes_local = field.shape[1]
    time_local = field.shape[2]
    table_re, table_im = dft_tables(RADIX)
    state = field.reshape(2, modes_local, time_local // RADIX, RADIX)
    state = to_columns(state)
    error_rows = []
    for step_index in range(STEPS):
        columns = state
        columns = linear_step(columns, beta, table_re, table_im)
        updated, error_part, field_part = kerr_step(
            columns.reshape(2, modes_local, time_local), quartets, intersections
        )
        error_sq, field_sq = lax.psum((error_part, field_part), "tm")
        error_rows.append(jnp.sqrt(error_sq / (field_sq + epsilon)))
        state = updated.reshape(columns.shape)
    state = to_rows(state)
    errors = jnp.stack(error_rows)
    return (state.reshape(2, modes_local, time_local), errors)


def solution(mesh):
    placed = (P(None, "mode", "tm"), P(None, "mode"), P(), P())
    return jax.shard_map(
        shards,
        mesh=mesh,
        in_specs=placed,
        out_specs=(P(None, "mode", "tm"), P(None, "mode")),
        check_vma=False,
    )
```

profile of v0, /device:TPU:18, one launch (start us, length us, event | category | flops | bytes accessed | tf_op | source)
XLA Modules:
  0.0 1882.4 jit_solution(8491664908036585077)
XLA Ops:
  18.4 44.6 %all-to-all-done = f32[4,1,131072]{2,1,0:T(1,128)S(1)} async-done(((f32[4,1,131072]{2,1,0:T(1,128)}), f32[4,1,131072]{2,1,0:T(1,128)S(1)}, u32[]{:S(2)}, u32[]{:S(2)}) %all-to-all-start) | async-done | bytes 2097184 | tf_op jit(solution)/shard_map/all_to_all | solution.py:42
  105.9 14.0 copy.160
  133.5 44.1 %all-to-all-done.1 = f32[4,1,131072]{2,1,0:T(1,128)} async-done(((f32[4,1,131072]{2,1,0:T(1,128)}), f32[4,1,131072]{2,1,0:T(1,128)}, u32[]{:S(2)}, u32[]{:S(2)}) %all-to-all-start.1) | async-done | bytes 2097184 | tf_op jit(solution)/shard_map/all_to_all | solution.py:69
  231.1 51.6 %all_to_all.174 = f32[4,1,131072]{2,1,0:T(1,128)} all-to-all(f32[4,1,131072]{2,1,0:T(1,128)S(1)} %reshape.495), channel_id=1, replica_groups=mesh['mode'=8,'tm'=4] {'tm'}, dimensions={0} | all-to-all | bytes 4194304 | tf_op jit(solution)/shard_map/all_to_all | solution.py:100
  322.2 14.8 copy.166
  337.0 24.7 %reshape.497 = f32[8,1,65536]{2,1,0:T(1,128)} reshape(f32[16384,2,16]{2,1,0:T(2,128)} %bitcast.446) | data formatting | bytes 4194304
  366.8 25.0 %all-to-all-done.3 = f32[8,1,65536]{2,1,0:T(1,128)} async-done(((f32[8,1,65536]{2,1,0:T(1,128)}), f32[8,1,65536]{2,1,0:T(1,128)}, u32[]{:S(2)}, u32[]{:S(2)}) %all-to-all-start.3) | async-done | bytes 2097184 | tf_op jit(solution)/shard_map/all_to_all | solution.py:141
  399.1 28.6 %reshape.498 = f32[16384,2,16]{2,1,0:T(2,128)} reshape(f32[8,65536]{1,0:T(8,128)S(1)} %reduce.13) | data formatting | bytes 4194304
  427.7 21.6 %copy.201 = f32[2,16,8,2048]{3,1,2,0:T(8,128)} copy(f32[2,16,8,2048]{1,0,3,2:T(2,128)} %bitcast.447) | data formatting | bytes 4194304 | tf_op jit(solution)/shard_map/all_to_all | solution.py:141
  452.5 210.8 %while.44 = (s32[]{:T(128)}, f32[2,128,2048]{2,1,0:T(8,128)}, s32[2,4,512]{2,1,0:T(4,128)S(1)}, f32[2,512]{1,0:T(2,128)S(1)}, f32[2,128,2048]{2,0,1:T(2,128)S(1)}, /*index=5*/s32[]{:T(128)}, s32[]{:T(128)}, s32[]{}, s32[]{}, s32[]{}) while((s32[]{:T(128)}, f32[2,128,2048]{2,1,0:T(8,128)}, s32[2,4,512]{2,1,0:T(4,128)S(1)}, ...), condition=%wide.region_1.3_spmd.clone, body=%wide.region_0.2_spmd.clone.sunk | while | flops 3243000320 | bytes 234956048 | solution.py:136
  453.0 19.4 %gather_fusion = f32[512,2,2048]{2,1,0:T(2,128)} fusion(f32[2,128,2048]{2,0,1:T(2,128)S(1)} %get-tuple-element.665, s32[1024]{0:T(1024)S(1)} %pad_clamp_fusion.24), kind=kCustom, calls=%fused_computation.1.clone.clone.1 | custom fusion | bytes 16779264 | tf_op jit(solution)/shard_map/while/body/eval_jaxpr/jit(_take)/gather | solution.py:128
  472.3 12.4 fusion.472
  484.7 19.5 %gather_fusion.1 = f32[512,2,2048]{2,1,0:T(2,128)} fusion(f32[2,128,2048]{2,0,1:T(2,128)S(1)} %get-tuple-element.665, s32[1024]{0:T(1024)S(1)} %pad_clamp_fusion.25), kind=kCustom, calls=%fused_computation.clone.clone.1 | custom fusion | bytes 16779264 | tf_op jit(solution)/shard_map/while/body/eval_jaxpr/jit(_take)/gather | solution.py:127
  504.3 9.2 fusion.473
  517.7 19.7 %gather_fusion.2 = f32[512,2,2048]{2,1,0:T(2,128)} fusion(f32[2,128,2048]{2,0,1:T(2,128)S(1)} %get-tuple-element.665, s32[1024]{0:T(1024)S(1)} %pad_clamp_fusion.26), kind=kCustom, calls=%fused_computation.2.clone.clone.1 | custom fusion | bytes 16779264 | tf_op jit(solution)/shard_map/while/body/eval_jaxpr/jit(_take)/gather | solution.py:129
  537.5 9.2 fusion.474
  556.7 19.4 %gather_fusion = f32[512,2,2048]{2,1,0:T(2,128)} fusion(f32[2,128,2048]{2,0,1:T(2,128)S(1)} %get-tuple-element.665, s32[1024]{0:T(1024)S(1)} %pad_clamp_fusion.24), kind=kCustom, calls=%fused_computation.1.clone.clone.1 | custom fusion | bytes 16779264 | tf_op jit(solution)/shard_map/while/body/eval_jaxpr/jit(_take)/gather | solution.py:128
  576.1 12.4 fusion.472
  588.5 19.8 %gather_fusion.1 = f32[512,2,2048]{2,1,0:T(2,128)} fusion(f32[2,128,2048]{2,0,1:T(2,128)S(1)} %get-tuple-element.665, s32[1024]{0:T(1024)S(1)} %pad_clamp_fusion.25), kind=kCustom, calls=%fused_computation.clone.clone.1 | custom fusion | bytes 16779264 | tf_op jit(solution)/shard_map/while/body/eval_jaxpr/jit(_take)/gather | solution.py:127
  608.2 9.2 fusion.473
  621.7 19.5 %gather_fusion.2 = f32[512,2,2048]{2,1,0:T(2,128)} fusion(f32[2,128,2048]{2,0,1:T(2,128)S(1)} %get-tuple-element.665, s32[1024]{0:T(1024)S(1)} %pad_clamp_fusion.26), kind=kCustom, calls=%fused_computation.2.clone.clone.1 | custom fusion | bytes 16779264 | tf_op jit(solution)/shard_map/while/body/eval_jaxpr/jit(_take)/gather | solution.py:129
  667.4 215.6 %while.45 = (s32[]{:T(128)}, f32[2,128,2048]{2,1,0:T(8,128)}, s32[2,4,512]{2,1,0:T(4,128)S(1)}, f32[2,512]{1,0:T(2,128)S(1)}, f32[2,128,2048]{2,0,1:T(2,128)S(1)}, /*index=5*/s32[]{:T(128)}, s32[]{:T(128)}, s32[]{}, s32[]{}, s32[]{}) while((s32[]{:T(128)}, f32[2,128,2048]{2,1,0:T(8,128)}, s32[2,4,512]{2,1,0:T(4,128)S(1)}, ...), condition=%wide.region_3.5_spmd.clone, body=%wide.region_2.4_spmd.clone.sunk | while | flops 3243000320 | bytes 234956048 | solution.py:136
  670.9 19.3 %gather_fusion.3 = f32[512,2,2048]{2,1,0:T(2,128)} fusion(f32[2,128,2048]{2,0,1:T(2,128)S(1)} %get-tuple-element.695, s32[1024]{0:T(1024)S(1)} %pad_clamp_fusion.27), kind=kCustom, calls=%fused_computation.4.clone.clone.1 | custom fusion | bytes 16779264 | tf_op jit(solution)/shard_map/while/body/eval_jaxpr/jit(_take)/gather | solution.py:128
  690.2 12.4 fusion.481
  702.6 19.8 %gather_fusion.4 = f32[512,2,2048]{2,1,0:T(2,128)} fusion(f32[2,128,2048]{2,0,1:T(2,128)S(1)} %get-tuple-element.695, s32[1024]{0:T(1024)S(1)} %pad_clamp_fusion.28), kind=kCustom, calls=%fused_computation.3.clone.clone.1 | custom fusion | bytes 16779264 | tf_op jit(solution)/shard_map/while/body/eval_jaxpr/jit(_take)/gather | solution.py:127
  722.4 9.2 fusion.482
  735.8 19.5 %gather_fusion.5 = f32[512,2,2048]{2,1,0:T(2,128)} fusion(f32[2,128,2048]{2,0,1:T(2,128)S(1)} %get-tuple-element.695, s32[1024]{0:T(1024)S(1)} %pad_clamp_fusion.29), kind=kCustom, calls=%fused_computation.5.clone.clone.1 | custom fusion | bytes 16779264 | tf_op jit(solution)/shard_map/while/body/eval_jaxpr/jit(_take)/gather | solution.py:129
  755.4 9.2 fusion.483
  774.8 19.3 %gather_fusion.3 = f32[512,2,2048]{2,1,0:T(2,128)} fusion(f32[2,128,2048]{2,0,1:T(2,128)S(1)} %get-tuple-element.695, s32[1024]{0:T(1024)S(1)} %pad_clamp_fusion.27), kind=kCustom, calls=%fused_computation.4.clone.clone.1 | custom fusion | bytes 16779264 | tf_op jit(solution)/shard_map/while/body/eval_jaxpr/jit(_take)/gather | solution.py:128
  794.2 12.4 fusion.481
  806.5 19.5 %gather_fusion.4 = f32[512,2,2048]{2,1,0:T(2,128)} fusion(f32[2,128,2048]{2,0,1:T(2,128)S(1)} %get-tuple-element.695, s32[1024]{0:T(1024)S(1)} %pad_clamp_fusion.28), kind=kCustom, calls=%fused_computation.3.clone.clone.1 | custom fusion | bytes 16779264 | tf_op jit(solution)/shard_map/while/body/eval_jaxpr/jit(_take)/gather | solution.py:127
  839.5 19.7 %gather_fusion.5 = f32[512,2,2048]{2,1,0:T(2,128)} fusion(f32[2,128,2048]{2,0,1:T(2,128)S(1)} %get-tuple-element.695, s32[1024]{0:T(1024)S(1)} %pad_clamp_fusion.29), kind=kCustom, calls=%fused_computation.5.clone.clone.1 | custom fusion | bytes 16779264 | tf_op jit(solution)/shard_map/while/body/eval_jaxpr/jit(_take)/gather | solution.py:129
  859.2 9.2 fusion.483
  889.7 29.1 %all_to_all.175 = f32[2,128,2048]{2,0,1:T(2,128)S(1)} all-to-all(f32[2,128,2048]{2,0,1:T(2,128)S(1)} %copy.171), channel_id=1, replica_groups=mesh['mode'=8,'tm'=4] {'mode'}, dimensions={1} | all-to-all | bytes 4194304 | tf_op jit(solution)/shard_map/all_to_all | solution.py:147
  956.1 51.8 %all_to_all.176 = f32[4,1,131072]{2,1,0:T(1,128)} all-to-all(f32[4,1,131072]{2,1,0:T(1,128)S(1)} %reshape.499), channel_id=1, replica_groups=mesh['mode'=8,'tm'=4] {'tm'}, dimensions={0} | all-to-all | bytes 4194304 | tf_op jit(solution)/shard_map/all_to_all | solution.py:69
  1061.5 51.0 %all_to_all.177 = f32[4,1,131072]{2,1,0:T(1,128)} all-to-all(f32[4,1,131072]{2,1,0:T(1,128)S(1)} %reshape.501), channel_id=1, replica_groups=mesh['mode'=8,'tm'=4] {'tm'}, dimensions={0} | all-to-all | bytes 4194304 | tf_op jit(solution)/shard_map/all_to_all | solution.py:100
  1151.6 14.8 copy.183
  1166.4 24.8 %reshape.503 = f32[8,1,65536]{2,1,0:T(1,128)} reshape(f32[16384,2,16]{2,1,0:T(2,128)} %bitcast.448) | data formatting | bytes 4194304
  1198.9 22.2 %all-to-all-done.7 = f32[8,1,65536]{2,1,0:T(1,128)} async-done(((f32[8,1,65536]{2,1,0:T(1,128)}), f32[8,1,65536]{2,1,0:T(1,128)}, u32[]{:S(2)}, u32[]{:S(2)}) %all-to-all-start.7) | async-done | bytes 2097184 | tf_op jit(solution)/shard_map/all_to_all | solution.py:141
  1234.4 28.7 %reshape.504 = f32[16384,2,16]{2,1,0:T(2,128)} reshape(f32[8,65536]{1,0:T(8,128)S(1)} %reduce.16) | data formatting | bytes 4194304
  1263.1 21.6 %copy.203 = f32[2,16,8,2048]{3,1,2,0:T(8,128)} copy(f32[2,16,8,2048]{1,0,3,2:T(2,128)} %bitcast.449) | data formatting | bytes 4194304 | tf_op jit(solution)/shard_map/all_to_all | solution.py:141
  1288.0 210.6 %while.46 = (s32[]{:T(128)}, f32[2,128,2048]{2,1,0:T(8,128)}, s32[2,4,512]{2,1,0:T(4,128)S(1)}, f32[2,512]{1,0:T(2,128)S(1)}, f32[2,128,2048]{2,0,1:T(2,128)S(1)}, /*index=5*/s32[]{:T(128)}, s32[]{:T(128)}, s32[]{}, s32[]{}, s32[]{}) while((s32[]{:T(128)}, f32[2,128,2048]{2,1,0:T(8,128)}, s32[2,4,512]{2,1,0:T(4,128)S(1)}, ...), condition=%wide.region_5.7_spmd.clone, body=%wide.region_4.6_spmd.clone.sunk | while | flops 3243000320 | bytes 234956048 | solution.py:136
  1288.2 19.3 %gather_fusion.6 = f32[512,2,2048]{2,1,0:T(2,128)} fusion(f32[2,128,2048]{2,0,1:T(2,128)S(1)} %get-tuple-element.725, s32[1024]{0:T(1024)S(1)} %pad_clamp_fusion.30), kind=kCustom, calls=%fused_computation.7.clone.clone.1 | custom fusion | bytes 16779264 | tf_op jit(solution)/shard_map/while/body/eval_jaxpr/jit(_take)/gather | solution.py:128
  1307.6 12.4 fusion.490
  1320.0 19.8 %gather_fusion.7 = f32[512,2,2048]{2,1,0:T(2,128)} fusion(f32[2,128,2048]{2,0,1:T(2,128)S(1)} %get-tuple-element.725, s32[1024]{0:T(1024)S(1)} %pad_clamp_fusion.31), kind=kCustom, calls=%fused_computation.6.clone.clone.1 | custom fusion | bytes 16779264 | tf_op jit(solution)/shard_map/while/body/eval_jaxpr/jit(_take)/gather | solution.py:127
  1339.8 9.2 fusion.491
  1353.2 19.5 %gather_fusion.8 = f32[512,2,2048]{2,1,0:T(2,128)} fusion(f32[2,128,2048]{2,0,1:T(2,128)S(1)} %get-tuple-element.725, s32[1024]{0:T(1024)S(1)} %pad_clamp_fusion.32), kind=kCustom, calls=%fused_computation.8.clone.clone.1 | custom fusion | bytes 16779264 | tf_op jit(solution)/shard_map/while/body/eval_jaxpr/jit(_take)/gather | solution.py:129
  1392.2 19.3 %gather_fusion.6 = f32[512,2,2048]{2,1,0:T(2,128)} fusion(f32[2,128,2048]{2,0,1:T(2,128)S(1)} %get-tuple-element.725, s32[1024]{0:T(1024)S(1)} %pad_clamp_fusion.30), kind=kCustom, calls=%fused_computation.7.clone.clone.1 | custom fusion | bytes 16779264 | tf_op jit(solution)/shard_map/while/body/eval_jaxpr/jit(_take)/gather | solution.py:128
  1411.5 12.4 fusion.490
  1424.0 19.5 %gather_fusion.7 = f32[512,2,2048]{2,1,0:T(2,128)} fusion(f32[2,128,2048]{2,0,1:T(2,128)S(1)} %get-tuple-element.725, s32[1024]{0:T(1024)S(1)} %pad_clamp_fusion.31), kind=kCustom, calls=%fused_computation.6.clone.clone.1 | custom fusion | bytes 16779264 | tf_op jit(solution)/shard_map/while/body/eval_jaxpr/jit(_take)/gather | solution.py:127
  1443.5 9.2 fusion.491
  1456.9 19.7 %gather_fusion.8 = f32[512,2,2048]{2,1,0:T(2,128)} fusion(f32[2,128,2048]{2,0,1:T(2,128)S(1)} %get-tuple-element.725, s32[1024]{0:T(1024)S(1)} %pad_clamp_fusion.32), kind=kCustom, calls=%fused_computation.8.clone.clone.1 | custom fusion | bytes 16779264 | tf_op jit(solution)/shard_map/while/body/eval_jaxpr/jit(_take)/gather | solution.py:129
  1476.6 9.2 fusion.492
  1502.7 229.3 %while.47 = (s32[]{:T(128)}, f32[2,128,2048]{2,1,0:T(8,128)}, s32[2,4,512]{2,1,0:T(4,128)S(1)}, f32[2,512]{1,0:T(2,128)S(1)}, f32[2,128,2048]{2,0,1:T(2,128)S(1)}, /*index=5*/s32[]{:T(128)}, s32[]{:T(128)}, s32[]{}, s32[]{}, s32[]{}) while((s32[]{:T(128)}, f32[2,128,2048]{2,1,0:T(8,128)}, s32[2,4,512]{2,1,0:T(4,128)S(1)}, ...), condition=%wide.region_7.9_spmd.clone, body=%wide.region_6.8_spmd.clone.sunk | while | flops 3243000320 | bytes 234956048 | solution.py:136
  1506.2 19.3 %gather_fusion.9 = f32[512,2,2048]{2,1,0:T(2,128)} fusion(f32[2,128,2048]{2,0,1:T(2,128)S(1)} %get-tuple-element.755, s32[1024]{0:T(1024)S(1)} %pad_clamp_fusion.33), kind=kCustom, calls=%fused_computation.10.clone.clone.1 | custom fusion | bytes 16779264 | tf_op jit(solution)/shard_map/while/body/eval_jaxpr/jit(_take)/gather | solution.py:128
  1525.5 12.4 fusion.499
  1538.0 30.0 %gather_fusion.10 = f32[512,2,2048]{2,1,0:T(2,128)} fusion(f32[2,128,2048]{2,0,1:T(2,128)S(1)} %get-tuple-element.755, s32[1024]{0:T(1024)S(1)} %pad_clamp_fusion.34), kind=kCustom, calls=%fused_computation.9.clone.clone.1 | custom fusion | bytes 16779264 | tf_op jit(solution)/shard_map/while/body/eval_jaxpr/jit(_take)/gather | solution.py:127
  1581.4 19.7 %gather_fusion.11 = f32[512,2,2048]{2,1,0:T(2,128)} fusion(f32[2,128,2048]{2,0,1:T(2,128)S(1)} %get-tuple-element.755, s32[1024]{0:T(1024)S(1)} %pad_clamp_fusion.35), kind=kCustom, calls=%fused_computation.11.clone.clone.1 | custom fusion | bytes 16779264 | tf_op jit(solution)/shard_map/while/body/eval_jaxpr/jit(_take)/gather | solution.py:129
  1620.3 19.3 %gather_fusion.9 = f32[512,2,2048]{2,1,0:T(2,128)} fusion(f32[2,128,2048]{2,0,1:T(2,128)S(1)} %get-tuple-element.755, s32[1024]{0:T(1024)S(1)} %pad_clamp_fusion.33), kind=kCustom, calls=%fused_computation.10.clone.clone.1 | custom fusion | bytes 16779264 | tf_op jit(solution)/shard_map/while/body/eval_jaxpr/jit(_take)/gather | solution.py:128
  1639.6 12.4 fusion.499
  1652.1 19.7 %gather_fusion.10 = f32[512,2,2048]{2,1,0:T(2,128)} fusion(f32[2,128,2048]{2,0,1:T(2,128)S(1)} %get-tuple-element.755, s32[1024]{0:T(1024)S(1)} %pad_clamp_fusion.34), kind=kCustom, calls=%fused_computation.9.clone.clone.1 | custom fusion | bytes 16779264 | tf_op jit(solution)/shard_map/while/body/eval_jaxpr/jit(_take)/gather | solution.py:127
  1685.2 19.5 %gather_fusion.11 = f32[512,2,2048]{2,1,0:T(2,128)} fusion(f32[2,128,2048]{2,0,1:T(2,128)S(1)} %get-tuple-element.755, s32[1024]{0:T(1024)S(1)} %pad_clamp_fusion.35), kind=kCustom, calls=%fused_computation.11.clone.clone.1 | custom fusion | bytes 16779264 | tf_op jit(solution)/shard_map/while/body/eval_jaxpr/jit(_take)/gather | solution.py:129
  1748.7 20.6 %all-to-all-done.8 = f32[2,128,2048]{2,0,1:T(2,128)S(1)} async-done(((f32[2,128,2048]{2,0,1:T(2,128)}), f32[2,128,2048]{2,0,1:T(2,128)S(1)}, u32[]{:S(2)}, u32[]{:S(2)}) %all-to-all-start.8) | async-done | bytes 2097184 | tf_op jit(solution)/shard_map/all_to_all | solution.py:147
  1817.5 39.8 %all-reduce = (f32[16]{0:T(128)S(1)}, f32[16]{0:T(128)S(1)}, f32[16]{0:T(128)S(1)}, f32[16]{0:T(128)S(1)}) all-reduce(f32[16]{0:T(128)S(1)} %reduce_sum.56, f32[16]{0:T(128)S(1)} %multiply_reduce_fusion, f32[16]{0:T(128)S(1)} %reduce_sum.52, f32[16]{0:T(128)S(1)} %multiply_reduce_fusion.2), channel_id=1, replica_groups=mesh['mode'=8,'tm'=4] {'tm'}, use_global_device_ids=true, to_apply=%region_15.17 | all-reduce | flops 64 | bytes 512 | tf_op jit(solution)/shard_map/psum | solution.py:168
  (364 shorter events, 620.2 us)
Async XLA Ops:
  12.9 50.1 %all-to-all-start = ((f32[4,1,131072]{2,1,0:T(1,128)}), f32[4,1,131072]{2,1,0:T(1,128)S(1)}, u32[]{:S(2)}, u32[]{:S(2)}) async-start(f32[4,1,131072]{2,1,0:T(1,128)} %reshape.491), calls=%async_computation | async-start | bytes 4194304 | tf_op jit(solution)/shard_map/all_to_all | solution.py:42
  18.4 86.7 %copy-start.27 = (f32[256,64]{0,1:T(8,128)}, f32[256,64]{0,1:T(8,128)S(1)}, u32[]{:S(2)}) copy-start(f32[256,64]{0,1:T(8,128)S(1)} %get-tuple-element.433) | copy-start | bytes 196612
  18.4 86.7 %copy-start.29 = (f32[256,64]{0,1:T(8,128)}, f32[256,64]{0,1:T(8,128)S(1)}, u32[]{:S(2)}) copy-start(f32[256,64]{0,1:T(8,128)S(1)} %get-tuple-element.434) | copy-start | bytes 196612
  63.0 1.3 copy-start.17
  101.1 4.1 copy-start.18
  101.1 4.1 copy-start.19
  119.9 13.2 copy-start.40
  125.4 52.2 %all-to-all-start.1 = ((f32[4,1,131072]{2,1,0:T(1,128)}), f32[4,1,131072]{2,1,0:T(1,128)}, u32[]{:S(2)}, u32[]{:S(2)}) async-start(f32[4,1,131072]{2,1,0:T(1,128)} %reshape.493), calls=%async_computation.1 | async-start | bytes 4194304 | tf_op jit(solution)/shard_map/all_to_all | solution.py:69
  133.1 74.7 %copy-start.33 = (f32[16]{0:T(128)}, f32[16]{0:T(128)S(1)}, u32[]{:S(2)}) copy-start(f32[16]{0:T(128)S(1)} %get-tuple-element.427) | copy-start | bytes 196
  133.1 74.7 %copy-start.35 = (f32[16]{0:T(128)}, f32[16]{0:T(128)S(1)}, u32[]{:S(2)}) copy-start(f32[16]{0:T(128)S(1)} %get-tuple-element.428) | copy-start | bytes 196
  133.1 74.7 %copy-start.37 = (f32[16]{0:T(128)}, f32[16]{0:T(128)S(1)}, u32[]{:S(2)}) copy-start(f32[16]{0:T(128)S(1)} %get-tuple-element.429) | copy-start | bytes 196
  133.5 74.3 %copy-start.25 = (f32[64,256]{1,0:T(8,128)}, f32[64,256]{1,0:T(8,128)S(1)}, u32[]{:S(2)}) copy-start(f32[64,256]{1,0:T(8,128)S(1)} %get-tuple-element.432) | copy-start | bytes 196612
  133.5 86.2 %copy-start.21 = (f32[64,256]{1,0:T(8,128)}, f32[64,256]{1,0:T(8,128)S(1)}, u32[]{:S(2)}) copy-start(f32[64,256]{1,0:T(8,128)S(1)} %get-tuple-element.430) | copy-start | bytes 196612
  133.5 86.2 %copy-start.23 = (f32[64,256]{1,0:T(8,128)}, f32[64,256]{1,0:T(8,128)S(1)}, u32[]{:S(2)}) copy-start(f32[64,256]{1,0:T(8,128)S(1)} %get-tuple-element.431) | copy-start | bytes 196612
  361.7 5.1 copy-start.39
  361.7 30.1 %all-to-all-start.3 = ((f32[8,1,65536]{2,1,0:T(1,128)}), f32[8,1,65536]{2,1,0:T(1,128)}, u32[]{:S(2)}, u32[]{:S(2)}) async-start(f32[8,1,65536]{2,1,0:T(1,128)} %reshape.497), calls=%async_computation.3 | async-start | bytes 4194304 | tf_op jit(solution)/shard_map/all_to_all | solution.py:141
  449.3 3.2 copy-start.20
  504.3 9.2 copy-start.8
  537.4 9.2 copy-start
  537.5 9.2 copy-start.1
  608.2 9.2 copy-start.8
  641.2 9.2 copy-start
  641.2 9.2 copy-start.1
  722.4 9.2 copy-start.9
  755.3 9.2 copy-start.2
  755.4 9.2 copy-start.3
  826.1 9.2 copy-start.9
  859.2 9.2 copy-start.2
  859.2 9.2 copy-start.3
  883.0 5.1 copy-start.31
  918.7 2.4 copy-start.13
  930.9 6.0 copy-start.12
  930.9 11.7 copy-start.28
  930.9 11.7 copy-start.30
  1031.3 6.9 copy-start.26
  1031.3 6.9 copy-start.34
  1031.3 6.9 copy-start.36
  1031.3 6.9 copy-start.38
  1044.0 6.1 copy-start.22
  1044.0 6.1 copy-start.24
  1191.2 4.7 copy-start.16
  1191.2 29.9 %all-to-all-start.7 = ((f32[8,1,65536]{2,1,0:T(1,128)}), f32[8,1,65536]{2,1,0:T(1,128)}, u32[]{:S(2)}, u32[]{:S(2)}) async-start(f32[8,1,65536]{2,1,0:T(1,128)} %reshape.503), calls=%async_computation.7 | async-start | bytes 4194304 | tf_op jit(solution)/shard_map/all_to_all | solution.py:141
  1221.1 518.9 %all-to-all-start.10 = ((f32[2,128,2048]{2,0,1:T(2,128)}), f32[2,128,2048]{2,0,1:T(2,128)}, u32[]{:S(2)}, u32[]{:S(2)}) async-start(f32[2,128,2048]{2,0,1:T(2,128)} %copy.193), calls=%async_computation.10 | async-start | bytes 4194304 | tf_op jit(solution)/shard_map/all_to_all | solution.py:148
  1284.7 3.2 copy-start.32
  1339.8 9.2 copy-start.10
  1372.7 9.2 copy-start.4
  1372.7 9.2 copy-start.5
  1443.5 9.2 copy-start.10
  1476.6 9.2 copy-start.4
  1476.6 9.2 copy-start.5
  1568.0 9.2 copy-start.11
  1601.1 9.2 copy-start.6
  1601.1 9.2 copy-start.7
  1671.8 9.2 copy-start.11
  1704.7 9.2 copy-start.6
  1704.7 9.2 copy-start.7
  1739.9 29.3 %all-to-all-start.8 = ((f32[2,128,2048]{2,0,1:T(2,128)}), f32[2,128,2048]{2,0,1:T(2,128)S(1)}, u32[]{:S(2)}, u32[]{:S(2)}) async-start(f32[2,128,2048]{2,0,1:T(2,128)} %copy.188), calls=%async_computation.8 | async-start | bytes 4194304 | tf_op jit(solution)/shard_map/all_to_all | solution.py:147
  1769.3 8.3 copy-start.15
  1769.3 31.0 %all-to-all-start.11 = ((f32[2,128,2048]{2,0,1:T(2,128)}), f32[2,128,2048]{2,0,1:T(2,128)}, u32[]{:S(2)}, u32[]{:S(2)}) async-start(f32[2,128,2048]{2,0,1:T(2,128)} %copy.194), calls=%async_computation.11 | async-start | bytes 4194304 | tf_op jit(solution)/shard_map/all_to_all | solution.py:148
  1794.5 16.0 copy-start.14
  1800.2 57.6 %all-to-all-start.9 = ((f32[4,1,131072]{2,1,0:T(1,128)}), f32[4,1,131072]{2,1,0:T(1,128)}, u32[]{:S(2)}, u32[]{:S(2)}) async-start(f32[4,1,131072]{2,1,0:T(1,128)} %reshape.505), calls=%async_computation.9 | async-start | bytes 4194304 | tf_op jit(solution)/shard_map/all_to_all | solution.py:46
where the time goes:
time: 1890 us; the launch traced here: 1880 us
  local copies, waits for them, and re-layouts  878 us (46%)
  other arithmetic  397 us (21%)
  blocking collectives  223 us (12%)
  waiting for transfers between devices  162 us (9%)
  matrix products  148 us (8%)
  starting transfers between devices  46.1 us (2%)
  loops' own time  25.8 us (1%)
    unnamed x79, local copies, waits for them, and re-layouts  174 us
    gather x8, local copies, waits for them, and re-layouts, accumulate(): jnp.take(fields, indices[1], axis=1)  168 us
    gather x8, local copies, waits for them, and re-layouts, accumulate(): jnp.take(fields, indices[3], axis=1)  157 us
    gather x8, local copies, waits for them, and re-layouts, accumulate(): jnp.take(fields, indices[2], axis=1)  155 us
    dot_general x44, matrix products, contract(): jnp.einsum(form, first_operand, second_operand, precision=lax.Precision.H...  138 us
    all_to_all x2, blocking collectives, linear_step(): lax.all_to_all(jnp.stack([back_re, back_im]), 'tm', split_axis=3, concat_...  103 us
    select_n x8, other arithmetic, accumulate(): jnp.take(fields, indices[2], axis=1)  99.3 us
    select_n x16, other arithmetic, accumulate(): jnp.take(fields, indices[3], axis=1)  73.6 us
  transfers between devices with their start and end apart: 8, of which 6 were waited for; matrix products, arithmetic and copies ran while one was open for 28% of the time, Pallas kernels for 0%

commit v1 on v0

--- a/solution.py
+++ b/solution.py
@@ -66,8 +66,14 @@
         * (row_position[:, None] * column[None, :] % total_time).astype(jnp.float32)
     )
     head_re, head_im = rotate(head_re, head_im, twist[None])
-    turned = lax.all_to_all(
-        jnp.stack([head_re, head_im]), "tm", split_axis=2, concat_axis=3, tiled=True
+    turned = jnp.concatenate(
+        lax.all_to_all(
+            jnp.stack(jnp.split(jnp.stack([head_re, head_im]), lax.axis_size("tm"), axis=2)),
+            "tm",
+            0,
+            0,
+        ),
+        axis=3,
     )
     spec_re = contract("mcb,kb->mck", turned[0], table_re) - contract(
         "mcb,kb->mck", turned[1], table_im

time: 1890 us -> 1910 us (1.011)
  no operation moved by 1% of the time
where the time goes in v1:
time: 1910 us; the launch traced here: 1900 us
  local copies, waits for them, and re-layouts  863 us (45%)
  other arithmetic  403 us (21%)
  blocking collectives  223 us (12%)
  waiting for transfers between devices  162 us (8%)
  matrix products  162 us (8%)
  starting transfers between devices  55.7 us (3%)
  loops' own time  25.8 us (1%)
    unnamed x79, local copies, waits for them, and re-layouts  174 us
    gather x8, local copies, waits for them, and re-layouts, accumulate(): jnp.take(fields, indices[1], axis=1)  168 us
    gather x8, local copies, waits for them, and re-layouts, accumulate(): jnp.take(fields, indices[3], axis=1)  157 us
    gather x8, local copies, waits for them, and re-layouts, accumulate(): jnp.take(fields, indices[2], axis=1)  155 us
    dot_general x44, matrix products, contract(): jnp.einsum(form, first_operand, second_operand, precision=lax.Precision.H...  152 us
    all_to_all x2, blocking collectives, linear_step(): lax.all_to_all(jnp.stack([back_re, back_im]), 'tm', split_axis=3, concat_...  103 us
    select_n x8, other arithmetic, accumulate(): jnp.take(fields, indices[2], axis=1)  99.4 us
    select_n x16, other arithmetic, accumulate(): jnp.take(fields, indices[3], axis=1)  73.6 us
  transfers between devices with their start and end apart: 8, of which 6 were waited for; matrix products, arithmetic and copies ran while one was open for 28% of the time, Pallas kernels for 0%

profile of v1, /device:TPU:18, one launch (start us, length us, event | category | flops | bytes accessed | tf_op | source)
XLA Modules:
  0.0 1896.1 jit_solution(9681170323607881498)
XLA Ops:
  18.4 44.6 %all-to-all-done = f32[4,1,131072]{2,1,0:T(1,128)S(1)} async-done(((f32[4,1,131072]{2,1,0:T(1,128)}), f32[4,1,131072]{2,1,0:T(1,128)S(1)}, u32[]{:S(2)}, u32[]{:S(2)}) %all-to-all-start) | async-done | bytes 2097184 | tf_op jit(solution)/shard_map/all_to_all | solution.py:42
  114.4 17.3 all-to-all-start.1
  132.1 44.0 %all-to-all-done.1 = f32[4,1,131072]{2,1,0:T(1,128)} async-done(((f32[4,1,131072]{2,1,0:T(1,128)}), f32[4,1,131072]{2,1,0:T(1,128)}, u32[]{:S(2)}, u32[]{:S(2)}) %all-to-all-start.1) | async-done | bytes 2097184 | tf_op jit(solution)/shard_map/all_to_all | solution.py:70
  231.4 51.7 %all_to_all.154 = f32[4,1,131072]{2,1,0:T(1,128)} all-to-all(f32[4,1,131072]{2,1,0:T(1,128)S(1)} %reshape.505), channel_id=1, replica_groups=mesh['mode'=8,'tm'=4] {'tm'}, dimensions={0} | all-to-all | bytes 4194304 | tf_op jit(solution)/shard_map/all_to_all | solution.py:106
  322.4 14.8 copy.162
  337.2 24.7 %reshape.507 = f32[8,1,65536]{2,1,0:T(1,128)} reshape(f32[16384,2,16]{2,1,0:T(2,128)} %bitcast.462) | data formatting | bytes 4194304
  367.1 25.0 %all-to-all-done.3 = f32[8,1,65536]{2,1,0:T(1,128)} async-done(((f32[8,1,65536]{2,1,0:T(1,128)}), f32[8,1,65536]{2,1,0:T(1,128)}, u32[]{:S(2)}, u32[]{:S(2)}) %all-to-all-start.3) | async-done | bytes 2097184 | tf_op jit(solution)/shard_map/all_to_all | solution.py:147
  399.3 28.6 %reshape.508 = f32[16384,2,16]{2,1,0:T(2,128)} reshape(f32[8,65536]{1,0:T(8,128)S(1)} %reduce.13) | data formatting | bytes 4194304
  427.9 21.6 %copy.197 = f32[2,16,8,2048]{3,1,2,0:T(8,128)} copy(f32[2,16,8,2048]{1,0,3,2:T(2,128)} %bitcast.463) | data formatting | bytes 4194304 | tf_op jit(solution)/shard_map/all_to_all | solution.py:147
  452.7 211.0 %while.44 = (s32[]{:T(128)}, f32[2,128,2048]{2,1,0:T(8,128)}, s32[2,4,512]{2,1,0:T(4,128)S(1)}, f32[2,512]{1,0:T(2,128)S(1)}, f32[2,128,2048]{2,0,1:T(2,128)S(1)}, /*index=5*/s32[]{:T(128)}, s32[]{:T(128)}, s32[]{}, s32[]{}, s32[]{}) while((s32[]{:T(128)}, f32[2,128,2048]{2,1,0:T(8,128)}, s32[2,4,512]{2,1,0:T(4,128)S(1)}, ...), condition=%wide.region_1.3_spmd.clone, body=%wide.region_0.2_spmd.clone.sunk | while | flops 3243000320 | bytes 234956048 | solution.py:142
  453.2 19.4 %gather_fusion = f32[512,2,2048]{2,1,0:T(2,128)} fusion(f32[2,128,2048]{2,0,1:T(2,128)S(1)} %get-tuple-element.673, s32[1024]{0:T(1024)S(1)} %pad_clamp_fusion.24), kind=kCustom, calls=%fused_computation.1.clone.clone.1 | custom fusion | bytes 16779264 | tf_op jit(solution)/shard_map/while/body/eval_jaxpr/jit(_take)/gather | solution.py:134
  472.5 12.4 fusion.488
  485.0 19.5 %gather_fusion.1 = f32[512,2,2048]{2,1,0:T(2,128)} fusion(f32[2,128,2048]{2,0,1:T(2,128)S(1)} %get-tuple-element.673, s32[1024]{0:T(1024)S(1)} %pad_clamp_fusion.25), kind=kCustom, calls=%fused_computation.clone.clone.1 | custom fusion | bytes 16779264 | tf_op jit(solution)/shard_map/while/body/eval_jaxpr/jit(_take)/gather | solution.py:133
  504.5 9.2 fusion.489
  517.9 19.7 %gather_fusion.2 = f32[512,2,2048]{2,1,0:T(2,128)} fusion(f32[2,128,2048]{2,0,1:T(2,128)S(1)} %get-tuple-element.673, s32[1024]{0:T(1024)S(1)} %pad_clamp_fusion.26), kind=kCustom, calls=%fused_computation.2.clone.clone.1 | custom fusion | bytes 16779264 | tf_op jit(solution)/shard_map/while/body/eval_jaxpr/jit(_take)/gather | solution.py:135
  537.7 9.2 fusion.490
  556.9 19.4 %gather_fusion = f32[512,2,2048]{2,1,0:T(2,128)} fusion(f32[2,128,2048]{2,0,1:T(2,128)S(1)} %get-tuple-element.673, s32[1024]{0:T(1024)S(1)} %pad_clamp_fusion.24), kind=kCustom, calls=%fused_computation.1.clone.clone.1 | custom fusion | bytes 16779264 | tf_op jit(solution)/shard_map/while/body/eval_jaxpr/jit(_take)/gather | solution.py:134
  576.3 12.4 fusion.488
  588.7 19.8 %gather_fusion.1 = f32[512,2,2048]{2,1,0:T(2,128)} fusion(f32[2,128,2048]{2,0,1:T(2,128)S(1)} %get-tuple-element.673, s32[1024]{0:T(1024)S(1)} %pad_clamp_fusion.25), kind=kCustom, calls=%fused_computation.clone.clone.1 | custom fusion | bytes 16779264 | tf_op jit(solution)/shard_map/while/body/eval_jaxpr/jit(_take)/gather | solution.py:133
  622.0 19.5 %gather_fusion.2 = f32[512,2,2048]{2,1,0:T(2,128)} fusion(f32[2,128,2048]{2,0,1:T(2,128)S(1)} %get-tuple-element.673, s32[1024]{0:T(1024)S(1)} %pad_clamp_fusion.26), kind=kCustom, calls=%fused_computation.2.clone.clone.1 | custom fusion | bytes 16779264 | tf_op jit(solution)/shard_map/while/body/eval_jaxpr/jit(_take)/gather | solution.py:135
  667.8 215.6 %while.45 = (s32[]{:T(128)}, f32[2,128,2048]{2,1,0:T(8,128)}, s32[2,4,512]{2,1,0:T(4,128)S(1)}, f32[2,512]{1,0:T(2,128)S(1)}, f32[2,128,2048]{2,0,1:T(2,128)S(1)}, /*index=5*/s32[]{:T(128)}, s32[]{:T(128)}, s32[]{}, s32[]{}, s32[]{}) while((s32[]{:T(128)}, f32[2,128,2048]{2,1,0:T(8,128)}, s32[2,4,512]{2,1,0:T(4,128)S(1)}, ...), condition=%wide.region_3.5_spmd.clone, body=%wide.region_2.4_spmd.clone.sunk | while | flops 3243000320 | bytes 234956048 | solution.py:142
  671.2 19.4 %gather_fusion.3 = f32[512,2,2048]{2,1,0:T(2,128)} fusion(f32[2,128,2048]{2,0,1:T(2,128)S(1)} %get-tuple-element.703, s32[1024]{0:T(1024)S(1)} %pad_clamp_fusion.27), kind=kCustom, calls=%fused_computation.4.clone.clone.1 | custom fusion | bytes 16779264 | tf_op jit(solution)/shard_map/while/body/eval_jaxpr/jit(_take)/gather | solution.py:134
  690.6 12.4 fusion.497
  703.0 19.8 %gather_fusion.4 = f32[512,2,2048]{2,1,0:T(2,128)} fusion(f32[2,128,2048]{2,0,1:T(2,128)S(1)} %get-tuple-element.703, s32[1024]{0:T(1024)S(1)} %pad_clamp_fusion.28), kind=kCustom, calls=%fused_computation.3.clone.clone.1 | custom fusion | bytes 16779264 | tf_op jit(solution)/shard_map/while/body/eval_jaxpr/jit(_take)/gather | solution.py:133
  736.2 19.5 %gather_fusion.5 = f32[512,2,2048]{2,1,0:T(2,128)} fusion(f32[2,128,2048]{2,0,1:T(2,128)S(1)} %get-tuple-element.703, s32[1024]{0:T(1024)S(1)} %pad_clamp_fusion.29), kind=kCustom, calls=%fused_computation.5.clone.clone.1 | custom fusion | bytes 16779264 | tf_op jit(solution)/shard_map/while/body/eval_jaxpr/jit(_take)/gather | solution.py:135
  755.8 9.2 fusion.499
  775.2 19.4 %gather_fusion.3 = f32[512,2,2048]{2,1,0:T(2,128)} fusion(f32[2,128,2048]{2,0,1:T(2,128)S(1)} %get-tuple-element.703, s32[1024]{0:T(1024)S(1)} %pad_clamp_fusion.27), kind=kCustom, calls=%fused_computation.4.clone.clone.1 | custom fusion | bytes 16779264 | tf_op jit(solution)/shard_map/while/body/eval_jaxpr/jit(_take)/gather | solution.py:134
  794.6 12.4 fusion.497
  807.0 19.5 %gather_fusion.4 = f32[512,2,2048]{2,1,0:T(2,128)} fusion(f32[2,128,2048]{2,0,1:T(2,128)S(1)} %get-tuple-element.703, s32[1024]{0:T(1024)S(1)} %pad_clamp_fusion.28), kind=kCustom, calls=%fused_computation.3.clone.clone.1 | custom fusion | bytes 16779264 | tf_op jit(solution)/shard_map/while/body/eval_jaxpr/jit(_take)/gather | solution.py:133
  826.5 9.2 fusion.498
  839.9 19.7 %gather_fusion.5 = f32[512,2,2048]{2,1,0:T(2,128)} fusion(f32[2,128,2048]{2,0,1:T(2,128)S(1)} %get-tuple-element.703, s32[1024]{0:T(1024)S(1)} %pad_clamp_fusion.29), kind=kCustom, calls=%fused_computation.5.clone.clone.1 | custom fusion | bytes 16779264 | tf_op jit(solution)/shard_map/while/body/eval_jaxpr/jit(_take)/gather | solution.py:135
  859.7 9.2 fusion.499
  890.1 29.1 %all_to_all.155 = f32[2,128,2048]{2,0,1:T(2,128)S(1)} all-to-all(f32[2,128,2048]{2,0,1:T(2,128)S(1)} %copy.167), channel_id=1, replica_groups=mesh['mode'=8,'tm'=4] {'mode'}, dimensions={1} | all-to-all | bytes 4194304 | tf_op jit(solution)/shard_map/all_to_all | solution.py:153
  937.2 18.8 fusion.148
  968.1 51.8 %all_to_all.156 = f32[4,1,131072]{2,1,0:T(1,128)} all-to-all(f32[4,1,131072]{2,1,0:T(1,128)S(1)} %reshape.509), channel_id=1, replica_groups=mesh['mode'=8,'tm'=4] {'tm'}, dimensions={0} | all-to-all | bytes 4194304 | tf_op jit(solution)/shard_map/all_to_all | solution.py:70
  1075.2 51.0 %all_to_all.157 = f32[4,1,131072]{2,1,0:T(1,128)} all-to-all(f32[4,1,131072]{2,1,0:T(1,128)S(1)} %reshape.511), channel_id=1, replica_groups=mesh['mode'=8,'tm'=4] {'tm'}, dimensions={0} | all-to-all | bytes 4194304 | tf_op jit(solution)/shard_map/all_to_all | solution.py:106
  1165.3 14.8 copy.179
  1180.1 24.8 %reshape.513 = f32[8,1,65536]{2,1,0:T(1,128)} reshape(f32[16384,2,16]{2,1,0:T(2,128)} %bitcast.464) | data formatting | bytes 4194304
  1212.6 22.2 %all-to-all-done.7 = f32[8,1,65536]{2,1,0:T(1,128)} async-done(((f32[8,1,65536]{2,1,0:T(1,128)}), f32[8,1,65536]{2,1,0:T(1,128)}, u32[]{:S(2)}, u32[]{:S(2)}) %all-to-all-start.7) | async-done | bytes 2097184 | tf_op jit(solution)/shard_map/all_to_all | solution.py:147
  1248.1 28.7 %reshape.514 = f32[16384,2,16]{2,1,0:T(2,128)} reshape(f32[8,65536]{1,0:T(8,128)S(1)} %reduce.16) | data formatting | bytes 4194304
  1276.8 21.6 %copy.199 = f32[2,16,8,2048]{3,1,2,0:T(8,128)} copy(f32[2,16,8,2048]{1,0,3,2:T(2,128)} %bitcast.465) | data formatting | bytes 4194304 | tf_op jit(solution)/shard_map/all_to_all | solution.py:147
  1301.6 210.7 %while.46 = (s32[]{:T(128)}, f32[2,128,2048]{2,1,0:T(8,128)}, s32[2,4,512]{2,1,0:T(4,128)S(1)}, f32[2,512]{1,0:T(2,128)S(1)}, f32[2,128,2048]{2,0,1:T(2,128)S(1)}, /*index=5*/s32[]{:T(128)}, s32[]{:T(128)}, s32[]{}, s32[]{}, s32[]{}) while((s32[]{:T(128)}, f32[2,128,2048]{2,1,0:T(8,128)}, s32[2,4,512]{2,1,0:T(4,128)S(1)}, ...), condition=%wide.region_5.7_spmd.clone, body=%wide.region_4.6_spmd.clone.sunk | while | flops 3243000320 | bytes 234956048 | solution.py:142
  1301.9 19.3 %gather_fusion.6 = f32[512,2,2048]{2,1,0:T(2,128)} fusion(f32[2,128,2048]{2,0,1:T(2,128)S(1)} %get-tuple-element.733, s32[1024]{0:T(1024)S(1)} %pad_clamp_fusion.30), kind=kCustom, calls=%fused_computation.7.clone.clone.1 | custom fusion | bytes 16779264 | tf_op jit(solution)/shard_map/while/body/eval_jaxpr/jit(_take)/gather | solution.py:134
  1321.2 12.5 fusion.506
  1333.7 19.8 %gather_fusion.7 = f32[512,2,2048]{2,1,0:T(2,128)} fusion(f32[2,128,2048]{2,0,1:T(2,128)S(1)} %get-tuple-element.733, s32[1024]{0:T(1024)S(1)} %pad_clamp_fusion.31), kind=kCustom, calls=%fused_computation.6.clone.clone.1 | custom fusion | bytes 16779264 | tf_op jit(solution)/shard_map/while/body/eval_jaxpr/jit(_take)/gather | solution.py:133
  1353.5 9.2 fusion.507
  1366.9 19.5 %gather_fusion.8 = f32[512,2,2048]{2,1,0:T(2,128)} fusion(f32[2,128,2048]{2,0,1:T(2,128)S(1)} %get-tuple-element.733, s32[1024]{0:T(1024)S(1)} %pad_clamp_fusion.32), kind=kCustom, calls=%fused_computation.8.clone.clone.1 | custom fusion | bytes 16779264 | tf_op jit(solution)/shard_map/while/body/eval_jaxpr/jit(_take)/gather | solution.py:135
  1386.4 9.2 fusion.508
  1405.9 19.3 %gather_fusion.6 = f32[512,2,2048]{2,1,0:T(2,128)} fusion(f32[2,128,2048]{2,0,1:T(2,128)S(1)} %get-tuple-element.733, s32[1024]{0:T(1024)S(1)} %pad_clamp_fusion.30), kind=kCustom, calls=%fused_computation.7.clone.clone.1 | custom fusion | bytes 16779264 | tf_op jit(solution)/shard_map/while/body/eval_jaxpr/jit(_take)/gather | solution.py:134
  1425.2 12.5 fusion.506
  1437.7 19.5 %gather_fusion.7 = f32[512,2,2048]{2,1,0:T(2,128)} fusion(f32[2,128,2048]{2,0,1:T(2,128)S(1)} %get-tuple-element.733, s32[1024]{0:T(1024)S(1)} %pad_clamp_fusion.31), kind=kCustom, calls=%fused_computation.6.clone.clone.1 | custom fusion | bytes 16779264 | tf_op jit(solution)/shard_map/while/body/eval_jaxpr/jit(_take)/gather | solution.py:133
  1457.2 9.2 fusion.507
  1470.6 19.7 %gather_fusion.8 = f32[512,2,2048]{2,1,0:T(2,128)} fusion(f32[2,128,2048]{2,0,1:T(2,128)S(1)} %get-tuple-element.733, s32[1024]{0:T(1024)S(1)} %pad_clamp_fusion.32), kind=kCustom, calls=%fused_computation.8.clone.clone.1 | custom fusion | bytes 16779264 | tf_op jit(solution)/shard_map/while/body/eval_jaxpr/jit(_take)/gather | solution.py:135
  1516.4 229.4 %while.47 = (s32[]{:T(128)}, f32[2,128,2048]{2,1,0:T(8,128)}, s32[2,4,512]{2,1,0:T(4,128)S(1)}, f32[2,512]{1,0:T(2,128)S(1)}, f32[2,128,2048]{2,0,1:T(2,128)S(1)}, /*index=5*/s32[]{:T(128)}, s32[]{:T(128)}, s32[]{}, s32[]{}, s32[]{}) while((s32[]{:T(128)}, f32[2,128,2048]{2,1,0:T(8,128)}, s32[2,4,512]{2,1,0:T(4,128)S(1)}, ...), condition=%wide.region_7.9_spmd.clone, body=%wide.region_6.8_spmd.clone.sunk | while | flops 3243000320 | bytes 234956048 | solution.py:142
  1519.9 19.3 %gather_fusion.9 = f32[512,2,2048]{2,1,0:T(2,128)} fusion(f32[2,128,2048]{2,0,1:T(2,128)S(1)} %get-tuple-element.763, s32[1024]{0:T(1024)S(1)} %pad_clamp_fusion.33), kind=kCustom, calls=%fused_computation.10.clone.clone.1 | custom fusion | bytes 16779264 | tf_op jit(solution)/shard_map/while/body/eval_jaxpr/jit(_take)/gather | solution.py:134
  1539.3 12.4 fusion.515
  1551.7 30.0 %gather_fusion.10 = f32[512,2,2048]{2,1,0:T(2,128)} fusion(f32[2,128,2048]{2,0,1:T(2,128)S(1)} %get-tuple-element.763, s32[1024]{0:T(1024)S(1)} %pad_clamp_fusion.34), kind=kCustom, calls=%fused_computation.9.clone.clone.1 | custom fusion | bytes 16779264 | tf_op jit(solution)/shard_map/while/body/eval_jaxpr/jit(_take)/gather | solution.py:133
  1595.2 19.7 %gather_fusion.11 = f32[512,2,2048]{2,1,0:T(2,128)} fusion(f32[2,128,2048]{2,0,1:T(2,128)S(1)} %get-tuple-element.763, s32[1024]{0:T(1024)S(1)} %pad_clamp_fusion.35), kind=kCustom, calls=%fused_computation.11.clone.clone.1 | custom fusion | bytes 16779264 | tf_op jit(solution)/shard_map/while/body/eval_jaxpr/jit(_take)/gather | solution.py:135
  1634.1 19.3 %gather_fusion.9 = f32[512,2,2048]{2,1,0:T(2,128)} fusion(f32[2,128,2048]{2,0,1:T(2,128)S(1)} %get-tuple-element.763, s32[1024]{0:T(1024)S(1)} %pad_clamp_fusion.33), kind=kCustom, calls=%fused_computation.10.clone.clone.1 | custom fusion | bytes 16779264 | tf_op jit(solution)/shard_map/while/body/eval_jaxpr/jit(_take)/gather | solution.py:134
  1653.4 12.4 fusion.515
  1665.9 19.7 %gather_fusion.10 = f32[512,2,2048]{2,1,0:T(2,128)} fusion(f32[2,128,2048]{2,0,1:T(2,128)S(1)} %get-tuple-element.763, s32[1024]{0:T(1024)S(1)} %pad_clamp_fusion.34), kind=kCustom, calls=%fused_computation.9.clone.clone.1 | custom fusion | bytes 16779264 | tf_op jit(solution)/shard_map/while/body/eval_jaxpr/jit(_take)/gather | solution.py:133
  1699.0 19.5 %gather_fusion.11 = f32[512,2,2048]{2,1,0:T(2,128)} fusion(f32[2,128,2048]{2,0,1:T(2,128)S(1)} %get-tuple-element.763, s32[1024]{0:T(1024)S(1)} %pad_clamp_fusion.35), kind=kCustom, calls=%fused_computation.11.clone.clone.1 | custom fusion | bytes 16779264 | tf_op jit(solution)/shard_map/while/body/eval_jaxpr/jit(_take)/gather | solution.py:135
  1762.5 20.6 %all-to-all-done.8 = f32[2,128,2048]{2,0,1:T(2,128)S(1)} async-done(((f32[2,128,2048]{2,0,1:T(2,128)}), f32[2,128,2048]{2,0,1:T(2,128)S(1)}, u32[]{:S(2)}, u32[]{:S(2)}) %all-to-all-start.8) | async-done | bytes 2097184 | tf_op jit(solution)/shard_map/all_to_all | solution.py:153
  1831.3 39.8 %all-reduce = (f32[16]{0:T(128)S(1)}, f32[16]{0:T(128)S(1)}, f32[16]{0:T(128)S(1)}, f32[16]{0:T(128)S(1)}) all-reduce(f32[16]{0:T(128)S(1)} %reduce_sum.56, f32[16]{0:T(128)S(1)} %multiply_reduce_fusion, f32[16]{0:T(128)S(1)} %reduce_sum.52, f32[16]{0:T(128)S(1)} %multiply_reduce_fusion.2), channel_id=1, replica_groups=mesh['mode'=8,'tm'=4] {'tm'}, use_global_device_ids=true, to_apply=%region_15.17 | all-reduce | flops 64 | bytes 512 | tf_op jit(solution)/shard_map/psum | solution.py:174
  (368 shorter events, 620.9 us)
Async XLA Ops:
  12.9 50.1 %all-to-all-start = ((f32[4,1,131072]{2,1,0:T(1,128)}), f32[4,1,131072]{2,1,0:T(1,128)S(1)}, u32[]{:S(2)}, u32[]{:S(2)}) async-start(f32[4,1,131072]{2,1,0:T(1,128)} %reshape.501), calls=%async_computation | async-start | bytes 4194304 | tf_op jit(solution)/shard_map/all_to_all | solution.py:42
  18.4 86.6 %copy-start.27 = (f32[256,64]{0,1:T(8,128)}, f32[256,64]{0,1:T(8,128)S(1)}, u32[]{:S(2)}) copy-start(f32[256,64]{0,1:T(8,128)S(1)} %get-tuple-element.441) | copy-start | bytes 196612
  18.4 86.6 %copy-start.29 = (f32[256,64]{0,1:T(8,128)}, f32[256,64]{0,1:T(8,128)S(1)}, u32[]{:S(2)}) copy-start(f32[256,64]{0,1:T(8,128)S(1)} %get-tuple-element.442) | copy-start | bytes 196612
  63.0 1.3 copy-start.17
  101.0 4.1 copy-start.18
  101.0 4.1 copy-start.19
  108.9 22.8 %copy-start.40 = (f32[3,16]{1,0:T(4,128)S(1)}, f32[3,16]{1,0:T(4,128)}, u32[]{:S(2)}) copy-start(f32[3,16]{1,0:T(4,128)} %param.15) | copy-start | bytes 580
  114.4 61.7 %all-to-all-start.1 = ((f32[4,1,131072]{2,1,0:T(1,128)}), f32[4,1,131072]{2,1,0:T(1,128)}, u32[]{:S(2)}, u32[]{:S(2)}) async-start(f32[4,1,131072]{2,1,0:T(1,128)} %reshape.503), calls=%async_computation.1 | async-start | bytes 4194304 | tf_op jit(solution)/shard_map/all_to_all | solution.py:70
  131.7 76.2 %copy-start.33 = (f32[16]{0:T(128)}, f32[16]{0:T(128)S(1)}, u32[]{:S(2)}) copy-start(f32[16]{0:T(128)S(1)} %get-tuple-element.435) | copy-start | bytes 196
  131.7 76.2 %copy-start.35 = (f32[16]{0:T(128)}, f32[16]{0:T(128)S(1)}, u32[]{:S(2)}) copy-start(f32[16]{0:T(128)S(1)} %get-tuple-element.436) | copy-start | bytes 196
  131.7 76.2 %copy-start.37 = (f32[16]{0:T(128)}, f32[16]{0:T(128)S(1)}, u32[]{:S(2)}) copy-start(f32[16]{0:T(128)S(1)} %get-tuple-element.437) | copy-start | bytes 196
  132.1 75.8 %copy-start.25 = (f32[64,256]{1,0:T(8,128)}, f32[64,256]{1,0:T(8,128)S(1)}, u32[]{:S(2)}) copy-start(f32[64,256]{1,0:T(8,128)S(1)} %get-tuple-element.440) | copy-start | bytes 196612
  132.1 87.9 %copy-start.21 = (f32[64,256]{1,0:T(8,128)}, f32[64,256]{1,0:T(8,128)S(1)}, u32[]{:S(2)}) copy-start(f32[64,256]{1,0:T(8,128)S(1)} %get-tuple-element.438) | copy-start | bytes 196612
  132.1 87.9 %copy-start.23 = (f32[64,256]{1,0:T(8,128)}, f32[64,256]{1,0:T(8,128)S(1)}, u32[]{:S(2)}) copy-start(f32[64,256]{1,0:T(8,128)S(1)} %get-tuple-element.439) | copy-start | bytes 196612
  362.0 5.1 copy-start.39
  362.0 30.2 %all-to-all-start.3 = ((f32[8,1,65536]{2,1,0:T(1,128)}), f32[8,1,65536]{2,1,0:T(1,128)}, u32[]{:S(2)}, u32[]{:S(2)}) async-start(f32[8,1,65536]{2,1,0:T(1,128)} %reshape.507), calls=%async_computation.3 | async-start | bytes 4194304 | tf_op jit(solution)/shard_map/all_to_all | solution.py:147
  449.5 3.2 copy-start.20
  504.5 9.2 copy-start.8
  537.7 9.2 copy-start
  537.7 9.2 copy-start.1
  608.5 9.2 copy-start.8
  641.5 9.2 copy-start
  641.5 9.2 copy-start.1
  722.8 9.2 copy-start.9
  755.7 9.2 copy-start.2
  755.7 9.2 copy-start.3
  826.5 9.2 copy-start.9
  859.7 9.2 copy-start.2
  859.7 9.2 copy-start.3
  883.4 5.1 copy-start.31
  919.2 2.4 copy-start.13
  931.2 6.0 copy-start.12
  931.2 24.8 %copy-start.28 = (f32[256,64]{0,1:T(8,128)S(1)}, f32[256,64]{0,1:T(8,128)}, u32[]{:S(2)}) copy-start(f32[256,64]{0,1:T(8,128)} %copy-done.27) | copy-start | bytes 196612
  931.2 24.8 %copy-start.30 = (f32[256,64]{0,1:T(8,128)S(1)}, f32[256,64]{0,1:T(8,128)}, u32[]{:S(2)}) copy-start(f32[256,64]{0,1:T(8,128)} %copy-done.29) | copy-start | bytes 196612
  1045.0 6.9 copy-start.26
  1045.0 6.9 copy-start.34
  1045.0 6.9 copy-start.36
  1045.0 6.9 copy-start.38
  1057.7 6.1 copy-start.22
  1057.7 6.1 copy-start.24
  1204.8 4.7 copy-start.16
  1204.8 29.9 %all-to-all-start.7 = ((f32[8,1,65536]{2,1,0:T(1,128)}), f32[8,1,65536]{2,1,0:T(1,128)}, u32[]{:S(2)}, u32[]{:S(2)}) async-start(f32[8,1,65536]{2,1,0:T(1,128)} %reshape.513), calls=%async_computation.7 | async-start | bytes 4194304 | tf_op jit(solution)/shard_map/all_to_all | solution.py:147
  1234.8 519.0 %all-to-all-start.10 = ((f32[2,128,2048]{2,0,1:T(2,128)}), f32[2,128,2048]{2,0,1:T(2,128)}, u32[]{:S(2)}, u32[]{:S(2)}) async-start(f32[2,128,2048]{2,0,1:T(2,128)} %copy.189), calls=%async_computation.10 | async-start | bytes 4194304 | tf_op jit(solution)/shard_map/all_to_all | solution.py:154
  1298.4 3.2 copy-start.32
  1353.5 9.2 copy-start.10
  1386.4 9.2 copy-start.4
  1386.4 9.2 copy-start.5
  1457.2 9.2 copy-start.10
  1490.3 9.2 copy-start.4
  1490.3 9.2 copy-start.5
  1581.8 9.2 copy-start.11
  1614.9 9.2 copy-start.6
  1614.9 9.2 copy-start.7
  1685.6 9.2 copy-start.11
  1718.5 9.2 copy-start.6
  1718.5 9.2 copy-start.7
  1753.8 29.3 %all-to-all-start.8 = ((f32[2,128,2048]{2,0,1:T(2,128)}), f32[2,128,2048]{2,0,1:T(2,128)S(1)}, u32[]{:S(2)}, u32[]{:S(2)}) async-start(f32[2,128,2048]{2,0,1:T(2,128)} %copy.184), calls=%async_computation.8 | async-start | bytes 4194304 | tf_op jit(solution)/shard_map/all_to_all | solution.py:153
  1783.1 8.3 copy-start.15
  1783.1 31.0 %all-to-all-start.11 = ((f32[2,128,2048]{2,0,1:T(2,128)}), f32[2,128,2048]{2,0,1:T(2,128)}, u32[]{:S(2)}, u32[]{:S(2)}) async-start(f32[2,128,2048]{2,0,1:T(2,128)} %copy.190), calls=%async_computation.11 | async-start | bytes 4194304 | tf_op jit(solution)/shard_map/all_to_all | solution.py:154
  1808.3 16.0 copy-start.14
  1814.1 57.6 %all-to-all-start.9 = ((f32[4,1,131072]{2,1,0:T(1,128)}), f32[4,1,131072]{2,1,0:T(1,128)}, u32[]{:S(2)}, u32[]{:S(2)}) async-start(f32[4,1,131072]{2,1,0:T(1,128)} %reshape.515), calls=%async_computation.9 | async-start | bytes 4194304 | tf_op jit(solution)/shard_map/all_to_all | solution.py:46
